TPU v7x, 128 devices: a whole 4x4x4 slice. The times are simulated.
128 devices in a mesh: depth: 2 (over core), row: 16 (over z, x), col: 4 (over y).
Axes of the slice: x: 4, y: 4, z: 4, core: 2. Of those that a mesh axis runs over, the one named last changes fastest.
Arguments:
- right_side: bfloat16 [4, 16, 8, 128, 512], P(None, 'row', ('depth', 'col')), may hold values from -6 to 6
- inverse_diag: bfloat16 [4, 16, 8, 1, 128, 128], P(None, 'row', ('depth', 'col')), may hold values from -2 to 2.5, as said below
- coupling: bfloat16 [3, 16, 1024, 8, 2048], P(None, 'row', None, ('depth', 'col')), may hold values from -0.0625 to 0.0625
- pattern: int32 [3, 16, 8, 8, 16], P(None, 'row', None, ('depth', 'col')), may hold values 0 or 1
Outputs:
- forward_solution: bfloat16 [4, 16, 8, 128, 512], P(None, 'row', ('depth', 'col'))
- solution: bfloat16 [4, 16, 8, 128, 512], P(None, 'row', ('depth', 'col'))
Inputs may be any that keep to these rules, and one draw needn't show every extreme that they name: `inverse_diag`: each block is lower triangular with positive diagonal.
All inputs are finite; a program needn't handle non-finite values. No bound on the sum of `pattern` on one device may be relied on, other than what follows from the above.
Results may differ from a plain program's by a relative error of at most 0.025.
Values may be sent and summed in bfloat16 or wider, within the bound.
A program may use at most 128 MiB of HBM per device.

v0:
```python
import jax
import jax.numpy as jnp
from jax import lax
from jax.sharding import PartitionSpec as P


def apply_inverse(inverse, vector, transposed):
    blocks_in = vector.reshape(inverse.shape[0], inverse.shape[1], vector.shape[-1])
    einsum_form = "tji,tjn->tin" if transposed else "tij,tjn->tin"
    result = jnp.einsum(einsum_form, inverse, blocks_in, preferred_element_type=jnp.float32)
    return result.astype(jnp.bfloat16).reshape(vector.shape)


def lift_upward(masked, share_in):
    portion = lax.all_gather(share_in, "row", axis=0, tiled=True)
    span_rows = portion.shape[0] * portion.shape[2]
    return jnp.dot(
        masked, portion.reshape(span_rows, portion.shape[-1]), preferred_element_type=jnp.float32
    )


def carry_downward(masked, share_in):
    portion = lax.all_gather(share_in, ("depth", "col"), axis=1, tiled=True)
    span_rows = portion.shape[1] * portion.shape[2]
    return lax.dot_general(
        masked,
        portion.reshape(span_rows, portion.shape[-1]),
        (((0,), (0,)), ((), ())),
        preferred_element_type=jnp.float32,
    )


def forward_sum(partial_value, share_rows):
    blocks = partial_value.reshape(
        lax.axis_size(("depth", "col")), share_rows, partial_value.shape[-1]
    )
    summed = lax.psum(blocks.astype(jnp.bfloat16), ("depth", "col")).astype(jnp.float32)
    return lax.dynamic_index_in_dim(summed, lax.axis_index(("depth", "col")), 0, keepdims=False)


def backward_sum(partial_value, share_rows):
    blocks = partial_value.reshape(lax.axis_size("row"), share_rows, partial_value.shape[-1])
    summed = lax.psum(blocks.astype(jnp.bfloat16), "row").astype(jnp.float32)
    return lax.dynamic_index_in_dim(summed, lax.axis_index("row"), 0, keepdims=False)


def body(right_side, inverse_diag, coupling, pattern):
    levels = right_side.shape[0]
    share_rows = right_side.shape[3]
    rhs_cols = right_side.shape[4]
    block_width = inverse_diag.shape[-1]
    masked = []
    for pair_at in range(levels - 1):
        slab = coupling[pair_at, 0, :, 0, :]
        gate = pattern[pair_at, 0, :, 0, :].astype(jnp.bfloat16)
        shaped = (
            slab.reshape(gate.shape[0], block_width, gate.shape[1], block_width)
            * gate[:, None, :, None]
        )
        masked.append(shaped.reshape(slab.shape))
    panel_spans = [(0, rhs_cols)]
    fwd_levels = []
    for level_at in range(levels):
        pieces = []
        for panel_at, (col_first, col_last) in enumerate(panel_spans):
            source = right_side[level_at, 0, 0, :, col_first:col_last]
            if level_at == 0:
                residual = source
            else:
                partial_value = lift_upward(
                    masked[level_at - 1], fwd_levels[level_at - 1][panel_at][None, None]
                )
                residual = (
                    source.astype(jnp.float32) - forward_sum(partial_value, share_rows)
                ).astype(jnp.bfloat16)
            pieces.append(apply_inverse(inverse_diag[level_at, 0, 0], residual, False))
        fwd_levels.append(pieces)
    bwd_levels = [None] * levels
    for level_at in reversed(range(levels)):
        pieces = []
        panel_at = 0
        known_part = fwd_levels[level_at][panel_at]
        if level_at == levels - 1:
            residual = known_part
        else:
            partial_value = carry_downward(
                masked[level_at], bwd_levels[level_at + 1][panel_at][None, None]
            )
            residual = (
                known_part.astype(jnp.float32) - backward_sum(partial_value, share_rows)
            ).astype(jnp.bfloat16)
        pieces.append(apply_inverse(inverse_diag[level_at, 0, 0], residual, True))
        bwd_levels[level_at] = pieces
    forward_rows = []
    backward_rows = []
    for level_at in range(levels):
        forward_rows.append(jnp.concatenate(fwd_levels[level_at], axis=1))
        backward_rows.append(jnp.concatenate(bwd_levels[level_at], axis=1))
    forward_solution = jnp.stack(forward_rows).reshape(levels, 1, 1, share_rows, rhs_cols)
    solution = jnp.stack(backward_rows).reshape(levels, 1, 1, share_rows, rhs_cols)
    return (forward_solution, solution)


def solution(mesh):
    placed = (
        P(None, "row", ("depth", "col"), None, None),
        P(None, "row", ("depth", "col"), None, None, None),
        P(None, "row", None, ("depth", "col"), None),
        P(None, "row", None, ("depth", "col"), None),
    )
    return jax.shard_map(
        body,
        mesh=mesh,
        in_specs=placed,
        out_specs=(
            P(None, "row", ("depth", "col"), None, None),
            P(None, "row", ("depth", "col"), None, None),
        ),
        check_vma=False,
    )
```

profile of v0, /device:TPU:0, one launch (start us, length us, event | category | flops | bytes accessed | tf_op | source)
XLA Modules:
  0.0 735.9 jit_solution(18099699853977080136)
XLA Ops:
  7.2 1.8 convolution_convert_fusion.10
  9.8 2.6 mul.62
  12.3 7.3 mul.63
  19.6 2.6 mul.71
  22.2 7.3 mul.72
  29.6 2.6 mul.67
  32.2 7.4 mul.68
  39.5 13.6 %slice_multiply_fusion.2 = (bf16[1,1,1024,1,2048]{4,2,3,1,0:T(8,128)(2,1)}, bf16[1,1,1024,1,2048]{4,2,3,1,0:T(8,128)(2,1)}, bf16[1,1,1024,1,2048]{4,2,3,1,0:T(8,128)(2,1)}) fusion(bf16[1,1,1024,1,2048]{4,2,3,1,0:T(8,128)(2,1)} %mul.63, bf16[3,1,1024,1,2048]{4,2,3,1,0:T(8,128)(2,1)} %param.6, bf16[1,1,1024,1,2048]{4,2,3,1,0:T(8,128)(2,1)} %mul.72, ...), kind=kLoop, calls=%fused_computation.8 | loop fusion | flops 6291456 | bytes 37748736 | tf_op jit(solution)/shard_map/mul | solution.py:57
  53.1 5.1 all-gather.13.cloned.1.call-done
  58.2 6.2 fusion.9
  64.5 62.1 %all-reduce.7.cloned.1.call-done = bf16[8,128,512]{2,1,0:T(8,128)(2,1)} async-done(((bf16[8,128,512]{2,1,0:T(8,128)(2,1)}), bf16[8,128,512]{2,1,0:T(8,128)(2,1)}) %all-reduce.7.cloned.1.call-update) | async-done | bytes 1048592 | tf_op jit(solution)/shard_map/psum | solution.py:37
  126.6 1.7 convolution_convert_fusion.5
  128.5 45.3 %all-gather.15.cloned.1.call-done = bf16[2048,512]{1,0:T(8,128)(2,1)} async-done(((bf16[128,512]{1,0:T(8,128)(2,1)}), bf16[2048,512]{1,0:T(8,128)(2,1)}) %all-gather.15.cloned.1.call-update) | async-done | bytes 2097168 | tf_op jit(solution)/shard_map/all_gather | solution.py:15
  173.7 6.2 fusion.12
  180.0 62.1 %all-reduce.9.cloned.1.call-done = bf16[8,128,512]{2,1,0:T(8,128)(2,1)} async-done(((bf16[8,128,512]{2,1,0:T(8,128)(2,1)}), bf16[8,128,512]{2,1,0:T(8,128)(2,1)}) %all-reduce.9.cloned.1.call-update) | async-done | bytes 1048592 | tf_op jit(solution)/shard_map/psum | solution.py:37
  243.9 44.5 %all-gather.17.cloned.1.call-done = bf16[2048,512]{1,0:T(8,128)(2,1)} async-done(((bf16[128,512]{1,0:T(8,128)(2,1)}), bf16[2048,512]{1,0:T(8,128)(2,1)}) %all-gather.17.cloned.1.call-update) | async-done | bytes 2097168 | tf_op jit(solution)/shard_map/all_gather | solution.py:15
  288.5 6.2 fusion.15
  294.7 62.1 %all-reduce.11.cloned.1.call-done = bf16[8,128,512]{2,1,0:T(8,128)(2,1)} async-done(((bf16[8,128,512]{2,1,0:T(8,128)(2,1)}), bf16[8,128,512]{2,1,0:T(8,128)(2,1)}) %all-reduce.11.cloned.1.call-update) | async-done | bytes 1048592 | tf_op jit(solution)/shard_map/psum | solution.py:37
  359.0 15.1 %fusion.2 = (bf16[2048,1024]{0,1:T(8,128)(2,1)}, bf16[2048,1024]{0,1:T(8,128)(2,1)}, bf16[2048,1024]{0,1:T(8,128)(2,1)}) fusion(bf16[128,8,16,128]{3,2,1,0:T(8,128)(2,1)} %bitcast.180, bf16[3,1,1024,1,2048]{4,2,3,1,0:T(8,128)(2,1)} %param.6, bf16[128,8,16,128]{3,2,1,0:T(8,128)(2,1)} %bitcast.182, bf16[128,8,16,128]{3,2,1,0:T(8,128)(2,1)} %bitcast.181), kind=kLoop, calls=%fused_computation.5 | loop fusion | flops 6291456 | bytes 37748736 | tf_op jit(solution)/shard_map/dot_general | solution.py:25
  374.1 6.4 copy.26
  381.6 6.3 convolution_convert_fusion.2
  387.9 92.3 %all-reduce.13.cloned.1.call-done = bf16[16,128,512]{2,1,0:T(8,128)(2,1)} async-done(((bf16[16,128,512]{2,1,0:T(8,128)(2,1)}), bf16[16,128,512]{2,1,0:T(8,128)(2,1)}) %all-reduce.13.cloned.1.call-update) | async-done | bytes 2097168 | tf_op jit(solution)/shard_map/psum | solution.py:43
  480.2 1.8 convolution_convert_fusion.8
  482.1 6.4 copy.25
  488.5 16.4 %all-gather.21.cloned.1.call-done = bf16[1024,512]{0,1:T(8,128)(2,1)} async-done(((bf16[128,512]{0,1:T(8,128)(2,1)}), bf16[1024,512]{0,1:T(8,128)(2,1)}) %all-gather.21.cloned.1.call-update) | async-done | bytes 1048592 | tf_op jit(solution)/shard_map/all_gather | solution.py:23
  504.9 6.3 convolution_convert_fusion.1
  511.2 92.3 %all-reduce.15.cloned.1.call-done = bf16[16,128,512]{2,1,0:T(8,128)(2,1)} async-done(((bf16[16,128,512]{2,1,0:T(8,128)(2,1)}), bf16[16,128,512]{2,1,0:T(8,128)(2,1)}) %all-reduce.15.cloned.1.call-update) | async-done | bytes 2097168 | tf_op jit(solution)/shard_map/psum | solution.py:43
  603.5 1.8 convolution_convert_fusion.7
  605.3 6.4 copy.24
  611.7 16.4 %all-gather.23.cloned.1.call-done = bf16[1024,512]{0,1:T(8,128)(2,1)} async-done(((bf16[128,512]{0,1:T(8,128)(2,1)}), bf16[1024,512]{0,1:T(8,128)(2,1)}) %all-gather.23.cloned.1.call-update) | async-done | bytes 1048592 | tf_op jit(solution)/shard_map/all_gather | solution.py:23
  628.2 6.3 convolution_convert_fusion
  635.3 91.5 %all-reduce.17.cloned.1.call-done = bf16[16,128,512]{2,1,0:T(8,128)(2,1)} async-done(((bf16[16,128,512]{2,1,0:T(8,128)(2,1)}), bf16[16,128,512]{2,1,0:T(8,128)(2,1)}) %all-reduce.17.cloned.1.call-update) | async-done | bytes 2097168 | tf_op jit(solution)/shard_map/psum | solution.py:43
  (50 shorter events, 9.4 us)
Async XLA Ops:
  7.2 51.1 %all-gather.13.cloned.1.call-start = ((), (), s32[]{:S(2)}) async-start(), calls=%async_computation.6 | async-start | bytes 2228224 | tf_op jit(solution)/shard_map/all_gather | solution.py:15
  9.0 117.6 %all-reduce.7.cloned.1.call-start = ((), (), s32[]{:S(2)}) async-start(), calls=%async_computation | async-start | bytes 2097152 | tf_op jit(solution)/shard_map/psum | solution.py:37
  58.2 68.4 %copy-start.6 = (bf16[4,1,1,128,512]{4,3,2,1,0:T(8,128)(2,1)S(1)}, bf16[4,1,1,128,512]{4,3,2,1,0:T(8,128)(2,1)}, u32[]{:S(2)}) copy-start(bf16[4,1,1,128,512]{4,3,2,1,0:T(8,128)(2,1)} %param.4) | copy-start | bytes 1572868
  58.2 68.4 %copy-start.7 = (bf16[4,1,1,1,128,128]{5,4,3,2,1,0:T(8,128)(2,1)S(1)}, bf16[4,1,1,1,128,128]{5,4,3,2,1,0:T(8,128)(2,1)}, u32[]{:S(2)}) copy-start(bf16[4,1,1,1,128,128]{5,4,3,2,1,0:T(8,128)(2,1)} %param.5) | copy-start | bytes 393220
  64.5 109.2 %all-gather.15.cloned.1.call-start = ((), (), s32[]{:S(2)}) async-start(), calls=%async_computation.7 | async-start | bytes 2228224 | tf_op jit(solution)/shard_map/all_gather | solution.py:15
  128.4 113.7 %all-reduce.9.cloned.1.call-start = ((), (), s32[]{:S(2)}) async-start(), calls=%async_computation.1 | async-start | bytes 2097152 | tf_op jit(solution)/shard_map/psum | solution.py:37
  180.0 108.5 %all-gather.17.cloned.1.call-start = ((), (), s32[]{:S(2)}) async-start(), calls=%async_computation.8 | async-start | bytes 2228224 | tf_op jit(solution)/shard_map/all_gather | solution.py:15
  243.9 113.0 %all-reduce.11.cloned.1.call-start = ((), (), s32[]{:S(2)}) async-start(), calls=%async_computation.2 | async-start | bytes 2097152 | tf_op jit(solution)/shard_map/psum | solution.py:37
  294.7 86.9 %all-gather.19.cloned.1.call-start = ((), (), s32[]{:S(2)}) async-start(), calls=%async_computation.9 | async-start | bytes 1179648 | tf_op jit(solution)/shard_map/all_gather | solution.py:23
  358.8 121.4 %all-reduce.13.cloned.1.call-start = ((), (), s32[]{:S(2)}) async-start(), calls=%async_computation.3 | async-start | bytes 4194304 | tf_op jit(solution)/shard_map/psum | solution.py:43
  381.6 98.7 %copy-start.2 = (bf16[512,128]{0,1:T(8,128)(2,1)S(1)}, bf16[512,128]{0,1:T(8,128)(2,1)}, u32[]{:S(2)}) copy-start(bf16[512,128]{0,1:T(8,128)(2,1)} %convolution_convert_fusion.4) | copy-start | bytes 393220
  387.9 117.0 %all-gather.21.cloned.1.call-start = ((), (), s32[]{:S(2)}) async-start(), calls=%async_computation.10 | async-start | bytes 1179648 | tf_op jit(solution)/shard_map/all_gather | solution.py:23
  482.0 121.4 %all-reduce.15.cloned.1.call-start = ((), (), s32[]{:S(2)}) async-start(), calls=%async_computation.4 | async-start | bytes 4194304 | tf_op jit(solution)/shard_map/psum | solution.py:43
  504.9 98.6 %copy-start.1 = (bf16[512,128]{0,1:T(8,128)(2,1)S(1)}, bf16[512,128]{0,1:T(8,128)(2,1)}, u32[]{:S(2)}) copy-start(bf16[512,128]{0,1:T(8,128)(2,1)} %convolution_convert_fusion.5) | copy-start | bytes 393220
  511.2 117.0 %all-gather.23.cloned.1.call-start = ((), (), s32[]{:S(2)}) async-start(), calls=%async_computation.11 | async-start | bytes 1179648 | tf_op jit(solution)/shard_map/all_gather | solution.py:23
  605.3 121.5 %all-reduce.17.cloned.1.call-start = ((), (), s32[]{:S(2)}) async-start(), calls=%async_computation.5 | async-start | bytes 4194304 | tf_op jit(solution)/shard_map/psum | solution.py:43
  628.1 6.3 copy-start
  628.1 99.8 %copy-start.3 = (bf16[512,128]{1,0:T(8,128)(2,1)S(1)}, bf16[512,128]{1,0:T(8,128)(2,1)}, u32[]{:S(2)}) copy-start(bf16[512,128]{1,0:T(8,128)(2,1)} %convolution_convert_fusion.9) | copy-start | bytes 393220
  628.1 99.8 %copy-start.4 = (bf16[512,128]{1,0:T(8,128)(2,1)S(1)}, bf16[512,128]{1,0:T(8,128)(2,1)}, u32[]{:S(2)}) copy-start(bf16[512,128]{1,0:T(8,128)(2,1)} %convolution_convert_fusion.8) | copy-start | bytes 393220
  628.2 99.8 %copy-start.5 = (bf16[512,128]{1,0:T(8,128)(2,1)S(1)}, bf16[512,128]{1,0:T(8,128)(2,1)}, u32[]{:S(2)}) copy-start(bf16[512,128]{1,0:T(8,128)(2,1)} %convolution_convert_fusion.7) | copy-start | bytes 393220
Sparse Core Ops, SparseCore 0:
  10.7 47.4 all-gather.12
  64.6 61.9 all-reduce.6
  129.4 44.3 all-gather.14
  180.1 61.9 all-reduce.8
  244.1 44.3 all-gather.16
  294.8 61.9 all-reduce.10
  358.9 22.6 all-gather.18
  388.0 92.1 all-reduce.12
  482.2 22.6 all-gather.20
  511.3 92.1 all-reduce.14
  605.4 22.6 all-gather.22
  634.6 92.1 all-reduce.16
where the time goes:
time: 737 us; the launch traced here: 736 us
  waiting for transfers between devices  591 us (80%)
  local copies, waits for them, and re-layouts  50 us (7%)
  matrix products  49.3 us (7%)
  other arithmetic  30.3 us (4%)
  between operations  14.3 us (2%)
    psum x3, waiting for transfers between devices, backward_sum(): summed = lax.psum(blocks.astype(jnp.bfloat16), 'row').astype(jnp.float32)  276 us
    psum x3, waiting for transfers between devices, forward_sum(): lax.psum(blocks.astype(jnp.bfloat16), ('depth', 'col')).astype(jnp.float32)  186 us
    all_gather x3, waiting for transfers between devices, lift_upward(): portion = lax.all_gather(share_in, 'row', axis=0, tiled=True)  94.9 us
    all_gather x3, waiting for transfers between devices, carry_downward(): portion = lax.all_gather(share_in, ('depth', 'col'), axis=1, tiled=True)  33.9 us
    mul x6, local copies, waits for them, and re-layouts, body(): slab.reshape(gate.shape[0], block_width, gate.shape[1], block_width)  29.7 us
    dot_general x3, local copies, waits for them, and re-layouts, carry_downward(): lax.dot_general(masked, portion.reshape(span_rows, portion.shape[-1]), ((...  19.2 us
    dot_general x3, matrix products, carry_downward(): lax.dot_general(masked, portion.reshape(span_rows, portion.shape[-1]), ((...  18.8 us
    dot_general x3, matrix products, lift_upward(): jnp.dot(masked, portion.reshape(span_rows, portion.shape[-1]), preferred_...  18.6 us
  transfers between devices with their start and end apart: 12, of which 12 were waited for; matrix products, arithmetic and copies ran while one was open for 11% of the time, Pallas kernels for 0%

commit v1 on v0

--- a/solution.py
+++ b/solution.py
@@ -1,7 +1,17 @@
+import functools
 import jax
 import jax.numpy as jnp
 from jax import lax
 from jax.sharding import PartitionSpec as P
+
+
+def process_the_trails(z_in, ax_name):
+    even = lax.all_gather(z_in, ax_name)
+    arr_out = jnp.sum(even, axis=0)
+    return arr_out
+
+
+_perform_record = functools.partial(process_the_trails, ax_name=("depth", "col"))
 
 
 def apply_inverse(inverse, vector, transposed):
@@ -34,7 +44,7 @@
     blocks = partial_value.reshape(
         lax.axis_size(("depth", "col")), share_rows, partial_value.shape[-1]
     )
-    summed = lax.psum(blocks.astype(jnp.bfloat16), ("depth", "col")).astype(jnp.float32)
+    summed = _perform_record(blocks.astype(jnp.bfloat16)).astype(jnp.float32)
     return lax.dynamic_index_in_dim(summed, lax.axis_index(("depth", "col")), 0, keepdims=False)
 
 

time: 737 us -> 712 us (0.966)
  waiting for transfers between devices: 591 us -> 554 us
  other arithmetic: 30.3 us -> 45.3 us
    psum x3 -> x0, waiting for transfers between devices: 186 us -> none  [forward_sum(): lax.psum(blocks.astype(jnp.bfloat16), ('depth', 'col')).astype(jnp.float32)]
    all_gather x0 -> x3, waiting for transfers between devices: none -> 147 us  [process_the_trails(): even = lax.all_gather(z_in, ax_name)]
    reduce_sum x0 -> x3, other arithmetic: none -> 15.1 us  [process_the_trails(): arr_out = jnp.sum(even, axis=0)]
where the time goes in v1:
time: 712 us; the launch traced here: 711 us
  waiting for transfers between devices  554 us (78%)
  local copies, waits for them, and re-layouts  49.9 us (7%)
  matrix products  46.5 us (7%)
  other arithmetic  45.3 us (6%)
  between operations  14.3 us (2%)
    psum x3, waiting for transfers between devices, backward_sum(): summed = lax.psum(blocks.astype(jnp.bfloat16), 'row').astype(jnp.float32)  276 us
    all_gather x3, waiting for transfers between devices, process_the_trails(): even = lax.all_gather(z_in, ax_name)  147 us
    all_gather x3, waiting for transfers between devices, lift_upward(): portion = lax.all_gather(share_in, 'row', axis=0, tiled=True)  95.7 us
    all_gather x3, waiting for transfers between devices, carry_downward(): portion = lax.all_gather(share_in, ('depth', 'col'), axis=1, tiled=True)  34.8 us
    mul x6, local copies, waits for them, and re-layouts, body(): slab.reshape(gate.shape[0], block_width, gate.shape[1], block_width)  29.7 us
    dot_general x3, local copies, waits for them, and re-layouts, carry_downward(): lax.dot_general(masked, portion.reshape(span_rows, portion.shape[-1]), ((...  19.2 us
    dot_general x3, matrix products, carry_downward(): lax.dot_general(masked, portion.reshape(span_rows, portion.shape[-1]), ((...  18.7 us
    dot_general x3, matrix products, lift_upward(): jnp.dot(masked, portion.reshape(span_rows, portion.shape[-1]), preferred_...  18.6 us
  transfers between devices with their start and end apart: 12, of which 12 were waited for; matrix products, arithmetic and copies ran while one was open for 11% of the time, Pallas kernels for 0%

profile of v1, /device:TPU:0, one launch (start us, length us, event | category | flops | bytes accessed | tf_op | source)
XLA Modules:
  0.0 710.7 jit_solution(8129723786512097328)
XLA Ops:
  9.8 2.6 mul.62
  12.4 7.3 %mul.63 = bf16[1,1,1024,1,2048]{4,2,3,1,0:T(8,128)(2,1)} reshape(bf16[8,128,16,128]{3,2,1,0:T(8,128)(2,1)} %mul.62) | data formatting | bytes 8388608 | tf_op jit(solution)/shard_map/mul | solution.py:67
  19.6 2.5 mul.71
  22.2 7.4 %mul.72 = bf16[1,1,1024,1,2048]{4,2,3,1,0:T(8,128)(2,1)} reshape(bf16[8,128,16,128]{3,2,1,0:T(8,128)(2,1)} %mul.71) | data formatting | bytes 8388608 | tf_op jit(solution)/shard_map/mul | solution.py:67
  29.6 2.6 mul.67
  32.1 7.3 %mul.68 = bf16[1,1,1024,1,2048]{4,2,3,1,0:T(8,128)(2,1)} reshape(bf16[8,128,16,128]{3,2,1,0:T(8,128)(2,1)} %mul.67) | data formatting | bytes 8388608 | tf_op jit(solution)/shard_map/mul | solution.py:67
  39.5 13.6 %slice_multiply_fusion.2 = (bf16[1,1,1024,1,2048]{4,2,3,1,0:T(8,128)(2,1)}, bf16[1,1,1024,1,2048]{4,2,3,1,0:T(8,128)(2,1)}, bf16[1,1,1024,1,2048]{4,2,3,1,0:T(8,128)(2,1)}) fusion(bf16[1,1,1024,1,2048]{4,2,3,1,0:T(8,128)(2,1)} %mul.63, bf16[3,1,1024,1,2048]{4,2,3,1,0:T(8,128)(2,1)} %param.6, bf16[1,1,1024,1,2048]{4,2,3,1,0:T(8,128)(2,1)} %mul.72, ...), kind=kLoop, calls=%fused_computation.8 | loop fusion | flops 6291456 | bytes 37748736 | tf_op jit(solution)/shard_map/mul | solution.py:67
  53.1 5.1 all-gather.19.cloned.1.call-done
  58.2 6.2 fusion.9
  64.5 49.0 %all-gather.21.cloned.1.call-done = bf16[64,128,512]{2,1,0:T(8,128)(2,1)} async-done(((bf16[8,128,512]{2,1,0:T(8,128)(2,1)}), bf16[64,128,512]{2,1,0:T(8,128)(2,1)}) %all-gather.21.cloned.1.call-update) | async-done | bytes 8388624 | tf_op jit(solution)/shard_map/all_gather | solution.py:9
  113.5 5.1 reduce_sum.36
  119.6 45.3 %all-gather.23.cloned.1.call-done = bf16[2048,512]{1,0:T(8,128)(2,1)} async-done(((bf16[128,512]{1,0:T(8,128)(2,1)}), bf16[2048,512]{1,0:T(8,128)(2,1)}) %all-gather.23.cloned.1.call-update) | async-done | bytes 2097168 | tf_op jit(solution)/shard_map/all_gather | solution.py:25
  164.8 6.2 fusion.12
  171.1 49.0 %all-gather.25.cloned.1.call-done = bf16[64,128,512]{2,1,0:T(8,128)(2,1)} async-done(((bf16[8,128,512]{2,1,0:T(8,128)(2,1)}), bf16[64,128,512]{2,1,0:T(8,128)(2,1)}) %all-gather.25.cloned.1.call-update) | async-done | bytes 8388624 | tf_op jit(solution)/shard_map/all_gather | solution.py:9
  220.2 5.0 reduce_sum.37
  226.1 45.3 %all-gather.27.cloned.1.call-done = bf16[2048,512]{1,0:T(8,128)(2,1)} async-done(((bf16[128,512]{1,0:T(8,128)(2,1)}), bf16[2048,512]{1,0:T(8,128)(2,1)}) %all-gather.27.cloned.1.call-update) | async-done | bytes 2097168 | tf_op jit(solution)/shard_map/all_gather | solution.py:25
  271.4 6.1 fusion.15
  277.8 48.9 %all-gather.29.cloned.1.call-done = bf16[64,128,512]{2,1,0:T(8,128)(2,1)} async-done(((bf16[8,128,512]{2,1,0:T(8,128)(2,1)}), bf16[64,128,512]{2,1,0:T(8,128)(2,1)}) %all-gather.29.cloned.1.call-update) | async-done | bytes 8388624 | tf_op jit(solution)/shard_map/all_gather | solution.py:9
  326.6 5.0 reduce_sum.38
  332.8 15.0 %fusion.2 = (bf16[2048,1024]{0,1:T(8,128)(2,1)}, bf16[2048,1024]{0,1:T(8,128)(2,1)}, bf16[2048,1024]{0,1:T(8,128)(2,1)}) fusion(bf16[128,8,16,128]{3,2,1,0:T(8,128)(2,1)} %bitcast.183, bf16[3,1,1024,1,2048]{4,2,3,1,0:T(8,128)(2,1)} %param.6, bf16[128,8,16,128]{3,2,1,0:T(8,128)(2,1)} %bitcast.185, bf16[128,8,16,128]{3,2,1,0:T(8,128)(2,1)} %bitcast.184), kind=kLoop, calls=%fused_computation.5 | loop fusion | flops 6291456 | bytes 37748736 | tf_op jit(solution)/shard_map/dot_general | solution.py:35
  347.8 6.4 copy.38
  354.1 2.2 all-gather.31.cloned.1.call-done
  356.3 6.2 convolution_convert_fusion.2
  362.6 92.3 %all-reduce.4.cloned.1.call-done = bf16[16,128,512]{2,1,0:T(8,128)(2,1)} async-done(((bf16[16,128,512]{2,1,0:T(8,128)(2,1)}), bf16[16,128,512]{2,1,0:T(8,128)(2,1)}) %all-reduce.4.cloned.1.call-update) | async-done | bytes 2097168 | tf_op jit(solution)/shard_map/psum | solution.py:53
  456.8 6.3 copy.37
  463.1 16.5 %all-gather.33.cloned.1.call-done = bf16[1024,512]{0,1:T(8,128)(2,1)} async-done(((bf16[128,512]{0,1:T(8,128)(2,1)}), bf16[1024,512]{0,1:T(8,128)(2,1)}) %all-gather.33.cloned.1.call-update) | async-done | bytes 1048592 | tf_op jit(solution)/shard_map/all_gather | solution.py:33
  479.6 6.3 convolution_convert_fusion.1
  485.9 92.3 %all-reduce.6.cloned.1.call-done = bf16[16,128,512]{2,1,0:T(8,128)(2,1)} async-done(((bf16[16,128,512]{2,1,0:T(8,128)(2,1)}), bf16[16,128,512]{2,1,0:T(8,128)(2,1)}) %all-reduce.6.cloned.1.call-update) | async-done | bytes 2097168 | tf_op jit(solution)/shard_map/psum | solution.py:53
  580.3 6.5 copy.36
  586.8 16.1 %all-gather.35.cloned.1.call-done = bf16[1024,512]{0,1:T(8,128)(2,1)} async-done(((bf16[128,512]{0,1:T(8,128)(2,1)}), bf16[1024,512]{0,1:T(8,128)(2,1)}) %all-gather.35.cloned.1.call-update) | async-done | bytes 1048592 | tf_op jit(solution)/shard_map/all_gather | solution.py:33
  602.9 6.3 convolution_convert_fusion
  610.1 91.5 %all-reduce.8.cloned.1.call-done = bf16[16,128,512]{2,1,0:T(8,128)(2,1)} async-done(((bf16[16,128,512]{2,1,0:T(8,128)(2,1)}), bf16[16,128,512]{2,1,0:T(8,128)(2,1)}) %all-reduce.8.cloned.1.call-update) | async-done | bytes 2097168 | tf_op jit(solution)/shard_map/psum | solution.py:53
  (53 shorter events, 12.9 us)
Async XLA Ops:
  7.2 51.1 %all-gather.19.cloned.1.call-start = ((), (), s32[]{:S(2)}) async-start(), calls=%async_computation.3 | async-start | bytes 2228224 | tf_op jit(solution)/shard_map/all_gather | solution.py:25
  9.0 104.5 %all-gather.21.cloned.1.call-start = ((), (), s32[]{:S(2)}) async-start(), calls=%async_computation.4 | async-start | bytes 9437184 | tf_op jit(solution)/shard_map/all_gather | solution.py:9
  64.5 100.4 %all-gather.23.cloned.1.call-start = ((), (), s32[]{:S(2)}) async-start(), calls=%async_computation.5 | async-start | bytes 2228224 | tf_op jit(solution)/shard_map/all_gather | solution.py:25
  113.5 5.1 copy-start.6
  113.5 5.1 copy-start.7
  119.5 100.6 %all-gather.25.cloned.1.call-start = ((), (), s32[]{:S(2)}) async-start(), calls=%async_computation.6 | async-start | bytes 9437184 | tf_op jit(solution)/shard_map/all_gather | solution.py:9
  171.1 100.3 %all-gather.27.cloned.1.call-start = ((), (), s32[]{:S(2)}) async-start(), calls=%async_computation.7 | async-start | bytes 2228224 | tf_op jit(solution)/shard_map/all_gather | solution.py:25
  226.0 100.6 %all-gather.29.cloned.1.call-start = ((), (), s32[]{:S(2)}) async-start(), calls=%async_computation.8 | async-start | bytes 9437184 | tf_op jit(solution)/shard_map/all_gather | solution.py:9
  277.6 78.8 %all-gather.31.cloned.1.call-start = ((), (), s32[]{:S(2)}) async-start(), calls=%async_computation.9 | async-start | bytes 1179648 | tf_op jit(solution)/shard_map/all_gather | solution.py:33
  332.7 122.2 %all-reduce.4.cloned.1.call-start = ((), (), s32[]{:S(2)}) async-start(), calls=%async_computation | async-start | bytes 4194304 | tf_op jit(solution)/shard_map/psum | solution.py:53
  356.3 98.6 %copy-start.2 = (bf16[512,128]{0,1:T(8,128)(2,1)S(1)}, bf16[512,128]{0,1:T(8,128)(2,1)}, u32[]{:S(2)}) copy-start(bf16[512,128]{0,1:T(8,128)(2,1)} %convolution_convert_fusion.4) | copy-start | bytes 393220
  362.6 117.0 %all-gather.33.cloned.1.call-start = ((), (), s32[]{:S(2)}) async-start(), calls=%async_computation.10 | async-start | bytes 1179648 | tf_op jit(solution)/shard_map/all_gather | solution.py:33
  456.7 121.5 %all-reduce.6.cloned.1.call-start = ((), (), s32[]{:S(2)}) async-start(), calls=%async_computation.1 | async-start | bytes 4194304 | tf_op jit(solution)/shard_map/psum | solution.py:53
  479.6 98.7 %copy-start.1 = (bf16[512,128]{0,1:T(8,128)(2,1)S(1)}, bf16[512,128]{0,1:T(8,128)(2,1)}, u32[]{:S(2)}) copy-start(bf16[512,128]{0,1:T(8,128)(2,1)} %convolution_convert_fusion.5) | copy-start | bytes 393220
  485.9 117.0 %all-gather.35.cloned.1.call-start = ((), (), s32[]{:S(2)}) async-start(), calls=%async_computation.11 | async-start | bytes 1179648 | tf_op jit(solution)/shard_map/all_gather | solution.py:33
  580.0 121.5 %all-reduce.8.cloned.1.call-start = ((), (), s32[]{:S(2)}) async-start(), calls=%async_computation.2 | async-start | bytes 4194304 | tf_op jit(solution)/shard_map/psum | solution.py:53
  602.9 6.3 copy-start
  602.9 99.8 %copy-start.3 = (bf16[512,128]{1,0:T(8,128)(2,1)S(1)}, bf16[512,128]{1,0:T(8,128)(2,1)}, u32[]{:S(2)}) copy-start(bf16[512,128]{1,0:T(8,128)(2,1)} %convolution_convert_fusion.9) | copy-start | bytes 393220
  602.9 99.8 %copy-start.4 = (bf16[512,128]{1,0:T(8,128)(2,1)S(1)}, bf16[512,128]{1,0:T(8,128)(2,1)}, u32[]{:S(2)}) copy-start(bf16[512,128]{1,0:T(8,128)(2,1)} %convolution_convert_fusion.8) | copy-start | bytes 393220
  602.9 99.8 %copy-start.5 = (bf16[512,128]{1,0:T(8,128)(2,1)S(1)}, bf16[512,128]{1,0:T(8,128)(2,1)}, u32[]{:S(2)}) copy-start(bf16[512,128]{1,0:T(8,128)(2,1)} %convolution_convert_fusion.7) | copy-start | bytes 393220
Sparse Core Ops, SparseCore 0:
  10.7 47.4 all-gather.18
  64.6 48.9 all-gather.20
  119.6 45.1 all-gather.22
  171.2 48.9 all-gather.24
  226.2 45.1 all-gather.26
  277.7 48.9 all-gather.28
  332.8 23.4 all-gather.30
  362.7 92.2 all-reduce.3
  456.9 22.6 all-gather.32
  486.0 92.1 all-reduce.5
  580.2 22.6 all-gather.34
  609.3 92.2 all-reduce.7
